TPU v7x, 1024 devices: a whole 8x8x8 slice. The times are simulated.
1024 devices in a mesh: prow: 16 (over y, x_lo), pcol: 64 (over z, x_hi, core).
Axes of the slice: x: 8 (x_hi: 4, x_lo: 2; x = x_hi * 2 + x_lo), y: 8, z: 8, core: 2. Of those that a mesh axis runs over, the one named last changes fastest.
Arguments:
- matrix: float32 [16384, 16384], P('prow', 'pcol'), may hold values from -6 to 6
- l_panels: float32 [2, 16384, 256], P(None, ('prow', 'pcol')), may hold values from -0.375 to 0.375
- l_inverse: float32 [2, 256, 256], replicated, as said below
- pivots: int32 [2, 256], replicated, may hold values from 0 to 16383, as said below
Outputs:
- updated: float32 [16384, 16384], P('prow', 'pcol')
Inputs may be any that keep to these rules, and one draw needn't show every extreme that they name: `pivots`: for each step s, entry k is either s * 256 + k or a row at or after (s + 1) * 256; the entries of one step are distinct. `l_inverse`: each block is unit lower triangular.
All inputs are finite; a program needn't handle non-finite values.
Results may differ from a plain program's by a relative error of at most 0.0001.
Values sent between devices are 32-bit elements; how exact they have to be, the bound alone decides.
A program may use at most 32 MiB of HBM per device.

v0:
```python
import jax
import jax.numpy as jnp
from jax import lax
from jax.sharding import PartitionSpec as P


def from_root(block, axis, source):
    block = jnp.where(lax.axis_index(axis) == source, block, jnp.zeros_like(block))
    return lax.psum(block, axis)


def per_device(matrix, l_panels, l_inverse, pivots):
    rows_dev = matrix.shape[0]
    first_row = lax.axis_index("prow") * rows_dev
    is_root = lax.axis_index("prow") == 0
    current = matrix
    for step in range(pivots.shape[0]):
        chosen = pivots[step]
        width = chosen.shape[0]
        begin = step * width
        offset = chosen - first_row
        owned = (offset >= 0) & (offset < rows_dev)
        clipped = jnp.clip(offset, 0, rows_dev - 1)
        own_rows = jnp.where(owned[:, None], current[clipped], jnp.float32(0.0))
        picked = lax.psum(own_rows, "prow")
        old_top = from_root(current[begin : begin + width], "prow", 0)
        target = jnp.where(owned, offset, rows_dev)
        current = current.at[target].set(old_top, mode="drop")
        product = jnp.dot(
            l_inverse[step],
            picked,
            precision=lax.Precision.HIGHEST,
            preferred_element_type=jnp.float32,
        )
        formed = jnp.where(is_root, product, jnp.float32(0.0))
        upper = from_root(formed, "prow", 0)
        kept_rows = current[begin : begin + width]
        current = current.at[begin : begin + width].set(jnp.where(is_root, upper, kept_rows))

        def apply_panel(piece, start, upper=upper, limit=begin + width):
            global_rows = first_row + jnp.arange(piece.shape[0], dtype=jnp.int32)
            factor = jnp.where((global_rows >= limit)[:, None], piece, jnp.float32(0.0))
            return jnp.dot(
                factor, upper, precision=lax.Precision.HIGHEST, preferred_element_type=jnp.float32
            )

        update = apply_panel(
            lax.all_gather(l_panels[step], "pcol", axis=0, tiled=True), jnp.int32(0)
        )
        current = current - update
    return current


def solution(mesh):
    placed = (P("prow", "pcol"), P(None, ("prow", "pcol"), None), P(), P())
    return jax.shard_map(
        per_device, mesh=mesh, in_specs=placed, out_specs=P("prow", "pcol"), check_vma=False
    )
```

profile of v0, /device:TPU:1, one launch (start us, length us, event | category | flops | bytes accessed | tf_op | source)
XLA Modules:
  0.0 638.7 jit_solution(9928261280661673367)
XLA Ops:
  7.4 1.2 copy.44
  8.6 0.7 copy-done.4
  9.3 1.0 gather_fusion
  10.3 0.8 broadcast_select_fusion.1
  11.1 0.0 all-reduce.13.cloned.1.call-start
  11.2 0.7 slice_select_fusion.1
  11.9 148.8 %all-reduce.7.cloned.1.call-done = f32[256,256]{1,0:T(8,128)} async-done(((f32[256,256]{1,0:T(8,128)}), f32[256,256]{1,0:T(8,128)}) %all-reduce.7.cloned.1.call-update) | async-done | bytes 262160 | tf_op jit(solution)/shard_map/psum | solution.py:25
  160.8 2.3 fusion.3
  163.1 0.0 all-gather.5.cloned.1.call-start
  163.1 0.7 copy-done.3
  163.8 0.6 fusion.16
  164.4 0.0 all-reduce.9.cloned.1.call-start
  164.5 150.2 %all-reduce.13.cloned.1.call-done = (f32[256,256]{1,0:T(8,128)}, f32[256,256]{0,1:T(8,128)}) async-done(((f32[256,256]{1,0:T(8,128)}, f32[256,256]{0,1:T(8,128)}), (f32[256,256]{1,0:T(8,128)}, f32[256,256]{0,1:T(8,128)})) %all-reduce.13.cloned.1.call-update) | async-done | bytes 524304 | tf_op jit(solution)/shard_map/psum | solution.py:9
  314.8 2.2 scatter_fusion
  317.0 0.1 copy.31
  317.2 0.8 copy-done
  318.0 0.1 copy.25
  318.2 2.3 convolution_subtract_fusion.1
  320.5 1.0 gather_fusion.1
  321.4 0.8 broadcast_select_fusion
  322.3 0.0 all-reduce.11.cloned.1.call-start
  322.3 0.7 slice_select_fusion
  323.1 148.2 %all-reduce.9.cloned.1.call-done = f32[256,256]{1,0:T(8,128)} async-done(((f32[256,256]{1,0:T(8,128)}), f32[256,256]{1,0:T(8,128)}) %all-reduce.9.cloned.1.call-update) | async-done | bytes 262160 | tf_op jit(solution)/shard_map/psum | solution.py:25
  471.3 2.3 fusion.1
  473.6 0.0 all-gather.7.cloned.1.call-start
  473.6 0.5 all-gather.7.cloned.1.call-update
  474.2 150.7 %all-reduce.11.cloned.1.call-done = (f32[256,256]{1,0:T(8,128)}, f32[256,256]{0,1:T(8,128)}) async-done(((f32[256,256]{1,0:T(8,128)}, f32[256,256]{0,1:T(8,128)}), (f32[256,256]{1,0:T(8,128)}, f32[256,256]{0,1:T(8,128)})) %all-reduce.11.cloned.1.call-update) | async-done | bytes 524304 | tf_op jit(solution)/shard_map/psum | solution.py:9
  624.9 2.2 scatter_fusion.1
  627.1 0.1 copy.32
  627.3 0.8 copy-done.1
  628.1 0.1 copy.30
  628.3 3.2 convolution_subtract_fusion
  (26 shorter events, 0.4 us)
Async XLA Ops:
  7.4 153.4 %all-reduce.7.cloned.1.call-start = ((), (), s32[]{:S(2)}) async-start(), calls=%async_computation | async-start | bytes 524288 | tf_op jit(solution)/shard_map/psum | solution.py:25
  8.6 0.7 copy-start.4
  11.1 149.7 %copy-start.2 = (f32[2,256,256]{2,1,0:T(8,128)S(1)}, f32[2,256,256]{2,1,0:T(8,128)}, u32[]{:S(2)}) copy-start(f32[2,256,256]{2,1,0:T(8,128)} %param.10) | copy-start | bytes 1572868
  11.1 303.6 %all-reduce.13.cloned.1.call-start = ((), (), s32[]{:S(2)}) async-start(), calls=%async_computation.5 | async-start | bytes 1048576 | tf_op jit(solution)/shard_map/psum | solution.py:9
  163.0 0.8 copy-start.3
  163.1 155.1 %all-gather.5.cloned.1.call-start = ((), (), s32[]{:S(2)}) async-start(), calls=%async_computation.2 | async-start | bytes 1064960 | tf_op jit(solution)/shard_map/all_gather | solution.py:48
  164.4 306.8 %all-reduce.9.cloned.1.call-start = ((), (), s32[]{:S(2)}) async-start(), calls=%async_computation.1 | async-start | bytes 524288 | tf_op jit(solution)/shard_map/psum | solution.py:25
  317.0 1.0 copy-start
  322.3 302.6 %all-reduce.11.cloned.1.call-start = ((), (), s32[]{:S(2)}) async-start(), calls=%async_computation.4 | async-start | bytes 1048576 | tf_op jit(solution)/shard_map/psum | solution.py:9
  473.6 154.7 %all-gather.7.cloned.1.call-start = ((), (), s32[]{:S(2)}) async-start(), calls=%async_computation.3 | async-start | bytes 1064960 | tf_op jit(solution)/shard_map/all_gather | solution.py:48
  627.1 1.0 copy-start.1
Sparse Core Ops, SparseCore 0:
  11.6 149.0 all-reduce.6
  164.3 150.4 all-reduce.12
  322.4 148.8 all-reduce.8
  474.7 150.1 all-reduce.10
Sparse Core Ops, SparseCore 1:
  168.1 102.5 all-gather.4
  478.6 102.5 all-gather.6
where the time goes:
time: 649 us; the launch traced here: 639 us
  waiting for transfers between devices  599 us (92%)
  between operations  14.8 us (2%)
  local copies, waits for them, and re-layouts  11.8 us (2%)
  matrix products  10 us (2%)
    psum x2, waiting for transfers between devices, from_root(): return lax.psum(block, axis)  301 us
    psum x2, waiting for transfers between devices, per_device(): picked = lax.psum(own_rows, 'prow')  297 us
  transfers between devices with their start and end apart: 6, of which 4 were waited for; matrix products, arithmetic and copies ran while one was open for 1% of the time, Pallas kernels for 0%

commit v1 on v0

v1 whole, which is shorter than its diff:
```python
import functools

import jax
import jax.numpy as jnp
from jax import lax
from jax.experimental import pallas as pl
from jax.experimental.pallas import tpu as pltpu
from jax.sharding import PartitionSpec as P

MESH = pl.DeviceIdType.MESH
HIGHEST = lax.Precision.HIGHEST
F32 = jnp.float32
BF16 = jnp.bfloat16


def split_cols(mesh):
    cols = mesh.shape["pcol"]
    core, xh = 2, (4 if cols >= 32 else 2)
    return cols // (core * xh), xh, core


def select(onehot, values):
    high = values.astype(BF16)
    rest = values - high.astype(F32)
    mid = rest.astype(BF16)
    low = (rest - mid.astype(F32)).astype(BF16)
    out = jnp.dot(onehot, high, preferred_element_type=F32)
    out = out + jnp.dot(onehot, mid, preferred_element_type=F32)
    return out + jnp.dot(onehot, low, preferred_element_type=F32)


def matmul(a, b):
    return jnp.dot(a, b, precision=HIGHEST, preferred_element_type=F32)


def kernel(
    sizes, a_ref, lp_ref, linv_ref, piv_ref, out_ref,
    rs_src, rs_dst, x_buf, t_buf, d_top, lf, z1, base,
    rs_s, rs_r, ag_s, ag_r, sc_s, sc_r, ta_s, ta_r,
    lx_s, lx_r, lz_s, lz_r, lc_s, lc_r, own_sem,
):
    rows_n, nz, nxh, nc, nb = sizes
    chunk = nb // rows_n
    blocks = a_ref.shape[0] // nb
    me = lax.axis_index("prow")
    col = lax.axis_index("pcol")
    core = lax.rem(col, nc)
    xh = lax.rem(col // nc, nxh)
    z = col // (nc * nxh)
    first = me * a_ref.shape[0]
    is_root = me == 0

    def row_peer(d):
        return lax.rem(me + d, rows_n)

    def xh_peer(d):
        return (z * nxh + lax.rem(xh + d, nxh)) * nc + core

    def z_peer(d):
        return (lax.rem(z + d, nz) * nxh + xh) * nc + core

    partner = (z * nxh + xh) * nc + (1 - core)

    def send(src, dst, s, r, **where):
        copy = pltpu.make_async_remote_copy(
            src_ref=src, dst_ref=dst, send_sem=s, recv_sem=r,
            device_id=where, device_id_type=MESH,
        )
        return copy

    barrier = pltpu.get_barrier_semaphore()
    for d in range(1, rows_n):
        pl.semaphore_signal(barrier, inc=1, device_id={"prow": row_peer(d)}, device_id_type=MESH)
    for d in range(1, nxh):
        pl.semaphore_signal(barrier, inc=1, device_id={"pcol": xh_peer(d)}, device_id_type=MESH)
    for d in range(1, nz):
        pl.semaphore_signal(barrier, inc=1, device_id={"pcol": z_peer(d)}, device_id_type=MESH)
    pl.semaphore_signal(barrier, inc=1, device_id={"pcol": partner}, device_id_type=MESH)

    own = [
        pltpu.make_async_copy(lp_ref.at[s], lf.at[s, z * nxh + xh, core], own_sem.at[s])
        for s in range(2)
    ]
    own_t = pltpu.make_async_copy(
        a_ref.at[pl.ds(0, chunk)], t_buf.at[0, pl.ds(0, chunk)], own_sem.at[2]
    )
    for copy in own:
        copy.start()

    def as_row(s):
        return jnp.broadcast_to(piv_ref[pl.ds(s, 1), :], (nb, nb))

    row0, row1 = as_row(0), as_row(1)
    col0, col1 = row0.T, row1.T
    lane = lax.broadcasted_iota(jnp.int32, (nb, nb), 1)
    sub = lax.broadcasted_iota(jnp.int32, (nb, nb), 0)

    def source(wanted):
        hit = wanted == row0
        place = jnp.max(jnp.where(hit, lane, -1), axis=1, keepdims=True)
        place = jnp.broadcast_to(place, (nb, nb))
        return jnp.where(place >= 0, place, wanted)

    def pick(wanted):
        total = None
        for b in range(blocks):
            onehot = (wanted == lane + (first + b * nb)).astype(F32).astype(BF16)
            part = select(onehot, a_ref[pl.ds(b * nb, nb), :])
            total = part if total is None else total + part
        return total

    rs_src[0] = pick(col0).reshape(rows_n, chunk, -1)

    pl.semaphore_wait(barrier, (rows_n - 1) + (nxh - 1) + (nz - 1) + 1)

    waits = []

    lx = []
    for s in range(2):
        for d in range(1, nxh):
            copy = send(
                lp_ref.at[s], lf.at[s, z * nxh + xh, core], lx_s.at[s, d], lx_r.at[s, d],
                pcol=xh_peer(d),
            )
            copy.start()
            lx.append(copy)
    waits += lx

    def reduce_start(s):
        for d in range(1, rows_n):
            copy = send(
                rs_src.at[s, row_peer(d)], rs_dst.at[s, d], rs_s.at[s, d], rs_r.at[s, d],
                prow=row_peer(d),
            )
            copy.start()
            waits.append(copy)
        return waits[-(rows_n - 1):]

    def reduce_finish(s, copies):
        total = rs_src[s, me]
        for d in range(1, rows_n):
            copies[d - 1].wait_recv()
            total = total + rs_dst[s, d]
        mine = pl.ds(pl.multiple_of(me * chunk, chunk), chunk)
        x_buf[s, mine, :] = total

    def gather_start(buf, s, sems, r_sems):
        mine = pl.ds(pl.multiple_of(me * chunk, chunk), chunk)
        copies = []
        for d in range(1, rows_n):
            copy = send(
                buf.at[s, mine], buf.at[s, mine], sems.at[s, d], r_sems.at[s, d], prow=row_peer(d)
            )
            copy.start()
            copies.append(copy)
        waits.extend(copies)
        return copies

    def scatter_copies(src, s):
        copies = []
        for m in range(1, rows_n):
            rows = pl.ds(m * chunk, chunk)
            copies.append(
                send(src.at[rows], t_buf.at[s, rows], sc_s.at[s, m], sc_r.at[s], prow=jnp.int32(m))
            )
        return copies

    def scatter_wait(s):
        mine = pl.ds(pl.multiple_of(me * chunk, chunk), chunk)
        @pl.when(jnp.logical_not(is_root))
        def _():
            send(
                t_buf.at[s, mine], t_buf.at[s, mine], sc_s.at[s, 0], sc_r.at[s], prow=row_peer(1)
            ).wait_recv()

    rs0 = reduce_start(0)

    @pl.when(is_root)
    def _():
        own_t.start()
        for copy in scatter_copies(a_ref, 0):
            copy.start()

    z1[...] = pick(source(col1))

    @pl.when(is_root)
    def _():
        d_top[...] = pick(source(sub + nb))

    lz = [[], []]
    for s in range(2):
        own[s].wait()
        for d in range(1, nxh):
            lx[s * (nxh - 1) + d - 1].wait_recv()
        for d in range(1, nz):
            group = pl.ds(z * nxh, nxh)
            copy = send(
                lf.at[s, group, core], lf.at[s, group, core], lz_s.at[s, d], lz_r.at[s, d],
                pcol=z_peer(d),
            )
            copy.start()
            lz[s].append(copy)
    waits += lz[0] + lz[1]

    reduce_finish(0, rs0)
    ag0 = gather_start(x_buf, 0, ag_s, ag_r)

    scatter_wait(0)

    @pl.when(is_root)
    def _():
        own_t.wait()

    ta0 = gather_start(t_buf, 0, ta_s, ta_r)

    def panel_finish(s):
        for copy in lz[s]:
            copy.wait_recv()
        swap = send(
            lf.at[s, :, core], lf.at[s, :, core], lc_s.at[s], lc_r.at[s], pcol=partner
        )
        swap.start()
        swap.wait_recv()
        waits.append(swap)

    zb = nz // blocks

    def factor(s, b):
        per = nz * nxh // blocks
        return lf[s, pl.ds(b * per, per)].reshape(nb, nb)

    panel_finish(0)
    l_sel = None
    for b in range(blocks):
        onehot = (col1 == lane + (first + b * nb)).astype(F32).astype(BF16)
        part = select(onehot, factor(0, b))
        l_sel = part if l_sel is None else l_sel + part

    for copy in ag0:
        copy.wait_recv()
    upper0 = matmul(linv_ref[0], x_buf[0])
    rs_src[1] = (z1[...] - matmul(l_sel, upper0)).reshape(rows_n, chunk, -1)
    rs1 = reduce_start(1)

    @pl.when(is_root)
    def _():
        d_top[...] = d_top[...] - matmul(factor(0, 1), upper0)
        t_buf[1, pl.ds(0, chunk), :] = d_top[pl.ds(0, chunk), :]
        for copy in scatter_copies(d_top, 1):
            copy.start()

    for copy in ta0:
        copy.wait_recv()

    for b in range(blocks):
        here = sub + (first + b * nb)
        hit = (here == row0).astype(F32)
        moved = select(hit.astype(BF16), t_buf[0])
        any_hit = jnp.max(hit, axis=1, keepdims=True) > 0
        kept = jnp.where(any_hit, moved, a_ref[pl.ds(b * nb, nb), :])
        base[pl.ds(b * nb, nb), :] = kept - matmul(factor(0, b), upper0)

    reduce_finish(1, rs1)
    ag1 = gather_start(x_buf, 1, ag_s, ag_r)
    scatter_wait(1)
    ta1 = gather_start(t_buf, 1, ta_s, ta_r)

    panel_finish(1)

    for copy in ag1:
        copy.wait_recv()
    upper1 = matmul(linv_ref[1], x_buf[1])

    for copy in ta1:
        copy.wait_recv()
    for b in range(blocks):
        here = sub + (first + b * nb)
        hit = (here == row1).astype(F32)
        moved = select(hit.astype(BF16), t_buf[1])
        any_hit = jnp.max(hit, axis=1, keepdims=True) > 0
        value = jnp.where(any_hit, moved, base[pl.ds(b * nb, nb), :])
        value = value - matmul(factor(1, b), upper1)
        if b == 0:
            value = jnp.where(is_root, upper0, value)
        if b == 1:
            value = jnp.where(is_root, upper1, value)
        out_ref[pl.ds(b * nb, nb), :] = value

    for copy in waits:
        copy.wait_send()

    @pl.when(is_root)
    def _():
        for s, src in ((0, a_ref), (1, d_top)):
            for copy in scatter_copies(src, s):
                copy.wait_send()


def per_device(split, rows_n, matrix, l_panels, l_inverse, pivots):
    nz, nxh, nc = split
    rows_dev, cols_dev = matrix.shape
    nb = pivots.shape[1]
    chunk = nb // rows_n
    part = l_panels.shape[1]
    dma = pltpu.SemaphoreType.DMA
    vmem = pl.BlockSpec(memory_space=pltpu.VMEM)
    return pl.pallas_call(
        functools.partial(kernel, (rows_n, nz, nxh, nc, nb)),
        out_shape=jax.ShapeDtypeStruct(matrix.shape, F32),
        in_specs=[vmem] * 4,
        out_specs=vmem,
        scratch_shapes=[
            pltpu.VMEM((2, rows_n, chunk, cols_dev), F32),
            pltpu.VMEM((2, rows_n, chunk, cols_dev), F32),
            pltpu.VMEM((2, nb, cols_dev), F32),
            pltpu.VMEM((2, nb, cols_dev), F32),
            pltpu.VMEM((nb, cols_dev), F32),
            pltpu.VMEM((2, nz * nxh, nc, part, nb), F32),
            pltpu.VMEM((nb, cols_dev), F32),
            pltpu.VMEM((rows_dev, cols_dev), F32),
            dma((2, rows_n)), dma((2, rows_n)),
            dma((2, rows_n)), dma((2, rows_n)),
            dma((2, rows_n)), dma((2,)),
            dma((2, rows_n)), dma((2, rows_n)),
            dma((2, nxh)), dma((2, nxh)),
            dma((2, nz)), dma((2, nz)),
            dma((2,)), dma((2,)),
            dma((3,)),
        ],
        compiler_params=pltpu.CompilerParams(
            collective_id=0, has_side_effects=True, vmem_limit_bytes=48 * 1024 * 1024
        ),
    )(matrix, l_panels, l_inverse, pivots)


def solution(mesh):
    placed = (P("prow", "pcol"), P(None, ("prow", "pcol"), None), P(), P())
    body = functools.partial(per_device, split_cols(mesh), mesh.shape["prow"])
    return jax.shard_map(
        body, mesh=mesh, in_specs=placed, out_specs=P("prow", "pcol"), check_vma=False
    )
```

time: 649 us -> 77.7 us (0.12); the launches traced: 639 us -> 77.4 us
  waiting for transfers between devices: 599 us -> 0 us
  Pallas kernels: 0 us -> 72.7 us
  between operations: 14.8 us -> 0.01 us
  matrix products: 10 us -> 0 us
  local copies, waits for them, and re-layouts: 11.8 us -> 4.68 us
    psum x4 -> x0, waiting for transfers between devices: 598 us -> none  [the longest x2 301 us: from_root(): return lax.psum(block, axis)]
    pallas_call x0 -> x1, Pallas kernels: none -> 72.7 us  [per_device(): pl.pallas_call(functools.partial(kernel, (rows_n, nz, nxh, nc, nb)), out_...]
    dot_general x4 -> x0, matrix products: 10 us -> none  [the longest x2 5.48 us: apply_panel(): jnp.dot(factor, upper, precision=lax.Precision.HIGHEST, preferred_element...]
  transfers between devices with their start and end apart: 6 -> 0, of which waited for: 4 -> 0; matrix products, arithmetic and copies ran while one was open for 1% -> 0% of each run, Pallas kernels for 0% -> 0%
where the time goes in v1:
time: 77.7 us; the launch traced here: 77.4 us
  Pallas kernels  72.7 us (94%)
  local copies, waits for them, and re-layouts  4.68 us (6%)
    pallas_call x1, Pallas kernels, per_device(): pl.pallas_call(functools.partial(kernel, (rows_n, nz, nxh, nc, nb)), out_...  72.7 us
    unnamed x9, local copies, waits for them, and re-layouts  4.68 us

profile of v1, /device:TPU:1, one launch (start us, length us, event | category | flops | bytes accessed | tf_op | source)
XLA Modules:
  0.0 77.4 jit_solution(13778119186583464688)
XLA Ops:
  0.0 0.0 copy-start
  0.0 1.2 %copy-done = f32[1024,256]{1,0:T(8,128)S(1)} copy-done((f32[1024,256]{1,0:T(8,128)S(1)}, f32[1024,256]{1,0:T(8,128)}, u32[]{:S(2)}) %copy-start) | copy-done | bytes 1048600
  1.2 0.0 copy-start.1
  1.2 1.0 %copy-done.1 = f32[2,256,256]{2,1,0:T(8,128)S(1)} copy-done((f32[2,256,256]{2,1,0:T(8,128)S(1)}, f32[2,256,256]{2,1,0:T(8,128)}, u32[]{:S(2)}) %copy-start.1) | copy-done | bytes 524312
  2.3 0.0 copy-start.2
  2.3 0.8 copy-done.2
  3.0 0.0 copy-start.3
  3.0 0.7 copy-done.3
  3.7 72.7 %shard_map.46 = f32[1024,256]{1,0:T(8,128)S(1)} custom-call(f32[1024,256]{1,0:T(8,128)S(1)} %copy-done, f32[2,16,256]{2,1,0:T(8,128)S(1)} %copy-done.2, f32[2,256,256]{2,1,0:T(8,128)S(1)} %copy-done.1, s32[2,256]{1,0:T(2,128)S(1)} %copy-done.3), custom_call_target="tpu_custom_call" | custom-call | tf_op jit(solution)/shard_map/pallas_call | solution.py:307
  76.4 1.0 %copy.6 = f32[1024,256]{1,0:T(8,128)} copy(f32[1024,256]{1,0:T(8,128)S(1)} %shard_map.46) | data formatting | bytes 2097152
Async XLA Ops:
  0.0 1.2 %copy-start = (f32[1024,256]{1,0:T(8,128)S(1)}, f32[1024,256]{1,0:T(8,128)}, u32[]{:S(2)}) copy-start(f32[1024,256]{1,0:T(8,128)} %a_ref.1) | copy-start | bytes 3145732
  1.2 1.0 %copy-start.1 = (f32[2,256,256]{2,1,0:T(8,128)S(1)}, f32[2,256,256]{2,1,0:T(8,128)}, u32[]{:S(2)}) copy-start(f32[2,256,256]{2,1,0:T(8,128)} %linv_ref.1) | copy-start | bytes 1572868
  2.3 0.8 copy-start.2
  3.0 0.7 copy-start.3

commit v2 on v1

--- a/solution.py
+++ b/solution.py
@@ -14,9 +14,8 @@
 
 
 def split_cols(mesh):
-    cols = mesh.shape["pcol"]
-    core, xh = 2, (4 if cols >= 32 else 2)
-    return cols // (core * xh), xh, core
+    nz, core = 8, 2
+    return nz, mesh.shape["pcol"] // (nz * core), core
 
 
 def select(onehot, values):
@@ -34,16 +33,19 @@
 
 
 def kernel(
-    sizes, a_ref, lp_ref, linv_ref, piv_ref, out_ref,
+    sizes, a_hbm, lp_ref, linv_hbm, piv_hbm, out_ref,
+    a_ref, linv_ref, piv_ref,
     rs_src, rs_dst, x_buf, t_buf, d_top, lf, z1, base,
-    rs_s, rs_r, ag_s, ag_r, sc_s, sc_r, ta_s, ta_r,
-    lx_s, lx_r, lz_s, lz_r, lc_s, lc_r, own_sem,
+    rs_s, rs_r, ag_s, ag_r, sc_s, sc_r, ta_s, ta_r, tf_s, tf_r,
+    lx_s, lx_r, lz_s, lz_r, lc_s, lc_r, own_sem, in_sem,
 ):
     rows_n, nz, nxh, nc, nb = sizes
     chunk = nb // rows_n
+    ny = rows_n // 2
     blocks = a_ref.shape[0] // nb
     me = lax.axis_index("prow")
     col = lax.axis_index("pcol")
+    y, x = me // 2, lax.rem(me, 2)
     core = lax.rem(col, nc)
     xh = lax.rem(col // nc, nxh)
     z = col // (nc * nxh)
@@ -56,8 +58,13 @@
     def xh_peer(d):
         return (z * nxh + lax.rem(xh + d, nxh)) * nc + core
 
+    def z_at(d):
+        return lax.rem(z + d + nz, nz)
+
     def z_peer(d):
-        return (lax.rem(z + d, nz) * nxh + xh) * nc + core
+        return (z_at(d) * nxh + xh) * nc + core
+
+    far = sorted(range(1, rows_n), key=lambda d: -min(d, rows_n - d))
 
     partner = (z * nxh + xh) * nc + (1 - core)
 
@@ -73,7 +80,7 @@
         pl.semaphore_signal(barrier, inc=1, device_id={"prow": row_peer(d)}, device_id_type=MESH)
     for d in range(1, nxh):
         pl.semaphore_signal(barrier, inc=1, device_id={"pcol": xh_peer(d)}, device_id_type=MESH)
-    for d in range(1, nz):
+    for d in (1, -1, 2, -2):
         pl.semaphore_signal(barrier, inc=1, device_id={"pcol": z_peer(d)}, device_id_type=MESH)
     pl.semaphore_signal(barrier, inc=1, device_id={"pcol": partner}, device_id_type=MESH)
 
@@ -81,11 +88,16 @@
         pltpu.make_async_copy(lp_ref.at[s], lf.at[s, z * nxh + xh, core], own_sem.at[s])
         for s in range(2)
     ]
-    own_t = pltpu.make_async_copy(
-        a_ref.at[pl.ds(0, chunk)], t_buf.at[0, pl.ds(0, chunk)], own_sem.at[2]
-    )
-    for copy in own:
+    own_t = pltpu.make_async_copy(a_ref.at[pl.ds(0, chunk)], t_buf.at[0, 0, 0], own_sem.at[2])
+    loads = [
+        pltpu.make_async_copy(src, dst, in_sem.at[n])
+        for n, (src, dst) in enumerate(
+            ((piv_hbm, piv_ref), (a_hbm, a_ref), (linv_hbm, linv_ref))
+        )
+    ]
+    for copy in loads + own:
         copy.start()
+    loads[0].wait()
 
     def as_row(s):
         return jnp.broadcast_to(piv_ref[pl.ds(s, 1), :], (nb, nb))
@@ -109,9 +121,10 @@
             total = part if total is None else total + part
         return total
 
+    loads[1].wait()
     rs_src[0] = pick(col0).reshape(rows_n, chunk, -1)
 
-    pl.semaphore_wait(barrier, (rows_n - 1) + (nxh - 1) + (nz - 1) + 1)
+    pl.semaphore_wait(barrier, (rows_n - 1) + (nxh - 1) + 4 + 1)
 
     waits = []
 
@@ -127,51 +140,78 @@
     waits += lx
 
     def reduce_start(s):
-        for d in range(1, rows_n):
+        copies = []
+        for d in far:
             copy = send(
                 rs_src.at[s, row_peer(d)], rs_dst.at[s, d], rs_s.at[s, d], rs_r.at[s, d],
                 prow=row_peer(d),
             )
             copy.start()
-            waits.append(copy)
-        return waits[-(rows_n - 1):]
+            copies.append(copy)
+        waits.extend(copies)
+        return copies
 
     def reduce_finish(s, copies):
         total = rs_src[s, me]
-        for d in range(1, rows_n):
-            copies[d - 1].wait_recv()
+        for d, copy in reversed(list(zip(far, copies))):
+            copy.wait_recv()
             total = total + rs_dst[s, d]
         mine = pl.ds(pl.multiple_of(me * chunk, chunk), chunk)
         x_buf[s, mine, :] = total
 
-    def gather_start(buf, s, sems, r_sems):
+    def gather_start(s):
         mine = pl.ds(pl.multiple_of(me * chunk, chunk), chunk)
         copies = []
-        for d in range(1, rows_n):
+        for d in far:
             copy = send(
-                buf.at[s, mine], buf.at[s, mine], sems.at[s, d], r_sems.at[s, d], prow=row_peer(d)
+                x_buf.at[s, mine], x_buf.at[s, mine], ag_s.at[s, d], ag_r.at[s, d],
+                prow=row_peer(d),
             )
             copy.start()
             copies.append(copy)
         waits.extend(copies)
         return copies
+
+    def top_start(s):
+        copies = []
+        for d in sorted(range(1, ny), key=lambda d: -min(d, ny - d)):
+            piece = t_buf.at[s, y, x]
+            copy = send(
+                piece, piece, ta_s.at[s, d], ta_r.at[s, d], prow=lax.rem(y + d, ny) * 2 + x
+            )
+            copy.start()
+            copies.append(copy)
+        waits.extend(copies)
+        return copies
+
+    def top_forward(s, copies):
+        for copy in copies:
+            copy.wait_recv()
+        copy = send(
+            t_buf.at[s, :, x], t_buf.at[s, :, x], tf_s.at[s], tf_r.at[s], prow=y * 2 + 1 - x
+        )
+        copy.start()
+        waits.append(copy)
+        return copy
 
     def scatter_copies(src, s):
         copies = []
         for m in range(1, rows_n):
             rows = pl.ds(m * chunk, chunk)
             copies.append(
-                send(src.at[rows], t_buf.at[s, rows], sc_s.at[s, m], sc_r.at[s], prow=jnp.int32(m))
+                send(
+                    src.at[rows], t_buf.at[s, m // 2, m % 2], sc_s.at[s, m], sc_r.at[s],
+                    prow=jnp.int32(m),
+                )
             )
         return copies
 
     def scatter_wait(s):
-        mine = pl.ds(pl.multiple_of(me * chunk, chunk), chunk)
+        piece = t_buf.at[s, y, x]
+
         @pl.when(jnp.logical_not(is_root))
         def _():
-            send(
-                t_buf.at[s, mine], t_buf.at[s, mine], sc_s.at[s, 0], sc_r.at[s], prow=row_peer(1)
-            ).wait_recv()
+            send(piece, piece, sc_s.at[s, 0], sc_r.at[s], prow=row_peer(1)).wait_recv()
 
     rs0 = reduce_start(0)
 
@@ -185,25 +225,68 @@
 
     @pl.when(is_root)
     def _():
-        d_top[...] = pick(source(sub + nb))
-
-    lz = [[], []]
-    for s in range(2):
+        wanted = source(sub + nb)
+        onehot = (wanted == lane).astype(F32)
+        moved = select(onehot.astype(BF16), a_ref[pl.ds(0, nb), :])
+        swapped = jnp.max(onehot, axis=1, keepdims=True) > 0
+        d_top[...] = jnp.where(swapped, moved, a_ref[pl.ds(nb, nb), :])
+
+    turn = 1 - 2 * lax.rem(z, 2)
+    routes = (
+        (0, 1), (0, -1), (0, 2), (0, -2), (-2, 1), (2, -1), (-2 * turn, 2 * turn)
+    )
+
+    def z_copy(s, q):
+        held, there = routes[q]
+        group = lf.at[s, pl.ds(z_at(held) * nxh, nxh), core]
+        return send(group, group, lz_s.at[s, q], lz_r.at[s, q], pcol=z_peer(there))
+
+    def panel_x(s):
         own[s].wait()
-        for d in range(1, nxh):
-            lx[s * (nxh - 1) + d - 1].wait_recv()
-        for d in range(1, nz):
-            group = pl.ds(z * nxh, nxh)
-            copy = send(
-                lf.at[s, group, core], lf.at[s, group, core], lz_s.at[s, d], lz_r.at[s, d],
-                pcol=z_peer(d),
-            )
-            copy.start()
-            lz[s].append(copy)
-    waits += lz[0] + lz[1]
+        for copy in lx[s * (nxh - 1): (s + 1) * (nxh - 1)]:
+            copy.wait_recv()
+        copies = [z_copy(s, q) for q in (2, 3, 0, 1)]
+        for copy in copies:
+            copy.start()
+        waits.extend(copies)
+        return copies
+
+    def swap_start(s, offsets):
+        copies = []
+        for d in offsets:
+            group = lf.at[s, pl.ds(z_at(d) * nxh, nxh), core]
+            copies.append(
+                send(group, group, lc_s.at[s, d + 3], lc_r.at[s, d + 3], pcol=partner)
+            )
+            copies[-1].start()
+        waits.extend(copies)
+        return copies
+
+    def panel_pass(s, copies):
+        for copy in copies:
+            copy.wait_recv()
+        copies = [z_copy(s, q) for q in (6, 4, 5)]
+        for copy in copies:
+            copy.start()
+        waits.extend(copies)
+        return copies, swap_start(s, (0, -1, 1, -2, 2))
+
+    def panel_finish(s, copies, swaps):
+        for copy in copies:
+            copy.wait_recv()
+        swaps = swaps + swap_start(s, (4, -3, 3))
+        for copy in swaps:
+            copy.wait_recv()
+
+    def tops(s):
+        return t_buf[s].reshape(nb, -1)
+
+    lz0 = panel_x(0)
 
     reduce_finish(0, rs0)
-    ag0 = gather_start(x_buf, 0, ag_s, ag_r)
+    ag0 = gather_start(0)
+
+    lz0 = panel_pass(0, lz0)
 
     scatter_wait(0)
 
@@ -211,25 +294,14 @@
     def _():
         own_t.wait()
 
-    ta0 = gather_start(t_buf, 0, ta_s, ta_r)
-
-    def panel_finish(s):
-        for copy in lz[s]:
-            copy.wait_recv()
-        swap = send(
-            lf.at[s, :, core], lf.at[s, :, core], lc_s.at[s], lc_r.at[s], pcol=partner
-        )
-        swap.start()
-        swap.wait_recv()
-        waits.append(swap)
-
-    zb = nz // blocks
+    ta0 = top_start(0)
 
     def factor(s, b):
         per = nz * nxh // blocks
         return lf[s, pl.ds(b * per, per)].reshape(nb, nb)
 
-    panel_finish(0)
+    panel_finish(0, *lz0)
+    lz1 = panel_x(1)
     l_sel = None
     for b in range(blocks):
         onehot = (col1 == lane + (first + b * nb)).astype(F32).astype(BF16)
@@ -238,6 +310,7 @@
 
     for copy in ag0:
         copy.wait_recv()
+    loads[2].wait()
     upper0 = matmul(linv_ref[0], x_buf[0])
     rs_src[1] = (z1[...] - matmul(l_sel, upper0)).reshape(rows_n, chunk, -1)
     rs1 = reduce_start(1)
@@ -245,41 +318,51 @@
     @pl.when(is_root)
     def _():
         d_top[...] = d_top[...] - matmul(factor(0, 1), upper0)
-        t_buf[1, pl.ds(0, chunk), :] = d_top[pl.ds(0, chunk), :]
+        t_buf[1, 0, 0] = d_top[pl.ds(0, chunk), :]
         for copy in scatter_copies(d_top, 1):
             copy.start()
 
-    for copy in ta0:
-        copy.wait_recv()
+    tf0 = top_forward(0, ta0)
+    lz1 = panel_pass(1, lz1)
+    tf0.wait_recv()
 
     for b in range(blocks):
         here = sub + (first + b * nb)
         hit = (here == row0).astype(F32)
-        moved = select(hit.astype(BF16), t_buf[0])
+        moved = select(hit.astype(BF16), tops(0))
         any_hit = jnp.max(hit, axis=1, keepdims=True) > 0
         kept = jnp.where(any_hit, moved, a_ref[pl.ds(b * nb, nb), :])
         base[pl.ds(b * nb, nb), :] = kept - matmul(factor(0, b), upper0)
 
     reduce_finish(1, rs1)
-    ag1 = gather_start(x_buf, 1, ag_s, ag_r)
+    ag1 = gather_start(1)
     scatter_wait(1)
-    ta1 = gather_start(t_buf, 1, ta_s, ta_r)
-
-    panel_finish(1)
+    ta1 = top_start(1)
+
+    panel_finish(1, *lz1)
+
+    tf1 = top_forward(1, ta1)
 
     for copy in ag1:
         copy.wait_recv()
     upper1 = matmul(linv_ref[1], x_buf[1])
-
-    for copy in ta1:
-        copy.wait_recv()
+    upper1_high = upper1.astype(BF16)
+    upper1_low = (upper1 - upper1_high.astype(F32)).astype(BF16)
+
+    tf1.wait_recv()
     for b in range(blocks):
         here = sub + (first + b * nb)
         hit = (here == row1).astype(F32)
-        moved = select(hit.astype(BF16), t_buf[1])
+        moved = select(hit.astype(BF16), tops(1))
         any_hit = jnp.max(hit, axis=1, keepdims=True) > 0
         value = jnp.where(any_hit, moved, base[pl.ds(b * nb, nb), :])
-        value = value - matmul(factor(1, b), upper1)
+        left = factor(1, b)
+        high = left.astype(BF16)
+        low = (left - high.astype(F32)).astype(BF16)
+        change = jnp.dot(high, upper1_low, preferred_element_type=F32)
+        change = change + jnp.dot(low, upper1_high, preferred_element_type=F32)
+        change = change + jnp.dot(high, upper1_high, preferred_element_type=F32)
+        value = value - change
         if b == 0:
             value = jnp.where(is_root, upper0, value)
         if b == 1:
@@ -307,13 +390,16 @@
     return pl.pallas_call(
         functools.partial(kernel, (rows_n, nz, nxh, nc, nb)),
         out_shape=jax.ShapeDtypeStruct(matrix.shape, F32),
-        in_specs=[vmem] * 4,
+        in_specs=[pl.BlockSpec(memory_space=pl.ANY)] * 4,
         out_specs=vmem,
         scratch_shapes=[
+            pltpu.VMEM(matrix.shape, F32),
+            pltpu.VMEM(l_inverse.shape, F32),
+            pltpu.VMEM(pivots.shape, jnp.int32),
             pltpu.VMEM((2, rows_n, chunk, cols_dev), F32),
             pltpu.VMEM((2, rows_n, chunk, cols_dev), F32),
             pltpu.VMEM((2, nb, cols_dev), F32),
-            pltpu.VMEM((2, nb, cols_dev), F32),
+            pltpu.VMEM((2, rows_n // 2, 2, chunk, cols_dev), F32),
             pltpu.VMEM((nb, cols_dev), F32),
             pltpu.VMEM((2, nz * nxh, nc, part, nb), F32),
             pltpu.VMEM((nb, cols_dev), F32),
@@ -322,10 +408,11 @@
             dma((2, rows_n)), dma((2, rows_n)),
             dma((2, rows_n)), dma((2,)),
             dma((2, rows_n)), dma((2, rows_n)),
+            dma((2,)), dma((2,)),
             dma((2, nxh)), dma((2, nxh)),
             dma((2, nz)), dma((2, nz)),
-            dma((2,)), dma((2,)),
-            dma((3,)),
+            dma((2, nz)), dma((2, nz)),
+            dma((3,)), dma((3,)),
         ],
         compiler_params=pltpu.CompilerParams(
             collective_id=0, has_side_effects=True, vmem_limit_bytes=48 * 1024 * 1024

time: 77.7 us -> 75.1 us (0.967)
  Pallas kernels: 72.7 us -> 70.1 us
    pallas_call x1, Pallas kernels: 72.7 us -> 70.1 us  [per_device(): pl.pallas_call(functools.partial(kernel, (rows_n, nz, nxh, nc, nb)), out_...]
where the time goes in v2:
time: 75.1 us; the launch traced here: 74.8 us
  Pallas kernels  70.1 us (93%)
  local copies, waits for them, and re-layouts  4.68 us (6%)
    pallas_call x1, Pallas kernels, per_device(): pl.pallas_call(functools.partial(kernel, (rows_n, nz, nxh, nc, nb)), out_...  70.1 us
    unnamed x9, local copies, waits for them, and re-layouts  4.68 us

profile of v2, /device:TPU:1, one launch (start us, length us, event | category | flops | bytes accessed | tf_op | source)
XLA Modules:
  0.0 74.8 jit_solution(2225429205370759043)
XLA Ops:
  0.0 0.0 copy-start
  0.0 1.2 %copy-done = f32[1024,256]{1,0:T(8,128)S(1)} copy-done((f32[1024,256]{1,0:T(8,128)S(1)}, f32[1024,256]{1,0:T(8,128)}, u32[]{:S(2)}) %copy-start) | copy-done | bytes 1048600
  1.2 0.0 copy-start.1
  1.2 1.0 %copy-done.1 = f32[2,256,256]{2,1,0:T(8,128)S(1)} copy-done((f32[2,256,256]{2,1,0:T(8,128)S(1)}, f32[2,256,256]{2,1,0:T(8,128)}, u32[]{:S(2)}) %copy-start.1) | copy-done | bytes 524312
  2.3 0.0 copy-start.2
  2.3 0.8 %copy-done.2 = f32[2,16,256]{2,1,0:T(8,128)S(1)} copy-done((f32[2,16,256]{2,1,0:T(8,128)S(1)}, f32[2,16,256]{2,1,0:T(8,128)}, u32[]{:S(2)}) %copy-start.2) | copy-done | bytes 32792
  3.0 0.0 copy-start.3
  3.0 0.7 copy-done.3
  3.7 70.1 %shard_map.46 = f32[1024,256]{1,0:T(8,128)S(1)} custom-call(f32[1024,256]{1,0:T(8,128)S(1)} %copy-done, f32[2,16,256]{2,1,0:T(8,128)S(1)} %copy-done.2, f32[2,256,256]{2,1,0:T(8,128)S(1)} %copy-done.1, s32[2,256]{1,0:T(2,128)S(1)} %copy-done.3), custom_call_target="tpu_custom_call" | custom-call | tf_op jit(solution)/shard_map/pallas_call | solution.py:390
  73.8 1.0 %copy.6 = f32[1024,256]{1,0:T(8,128)} copy(f32[1024,256]{1,0:T(8,128)S(1)} %shard_map.46) | data formatting | bytes 2097152
Async XLA Ops:
  0.0 1.2 %copy-start = (f32[1024,256]{1,0:T(8,128)S(1)}, f32[1024,256]{1,0:T(8,128)}, u32[]{:S(2)}) copy-start(f32[1024,256]{1,0:T(8,128)} %a_hbm.1) | copy-start | bytes 3145732
  1.2 1.0 %copy-start.1 = (f32[2,256,256]{2,1,0:T(8,128)S(1)}, f32[2,256,256]{2,1,0:T(8,128)}, u32[]{:S(2)}) copy-start(f32[2,256,256]{2,1,0:T(8,128)} %linv_hbm.1) | copy-start | bytes 1572868
  2.3 0.8 %copy-start.2 = (f32[2,16,256]{2,1,0:T(8,128)S(1)}, f32[2,16,256]{2,1,0:T(8,128)}, u32[]{:S(2)}) copy-start(f32[2,16,256]{2,1,0:T(8,128)} %lp_ref.1) | copy-start | bytes 98308
  3.0 0.7 copy-start.3

commit v3 on v2

--- a/solution.py
+++ b/solution.py
@@ -11,6 +11,7 @@
 HIGHEST = lax.Precision.HIGHEST
 F32 = jnp.float32
 BF16 = jnp.bfloat16
+VMEM_LIMIT = 48 * 1024 * 1024
 
 
 def split_cols(mesh):
@@ -28,6 +29,17 @@
     return out + jnp.dot(onehot, low, preferred_element_type=F32)
 
 
+def split(values):
+    high = values.astype(BF16)
+    return high, (values - high.astype(F32)).astype(BF16)
+
+
+def product(a, b):
+    out = jnp.dot(a[0], b[1], preferred_element_type=F32)
+    out = out + jnp.dot(a[1], b[0], preferred_element_type=F32)
+    return out + jnp.dot(a[0], b[0], preferred_element_type=F32)
+
+
 def matmul(a, b):
     return jnp.dot(a, b, precision=HIGHEST, preferred_element_type=F32)
 
@@ -35,9 +47,9 @@
 def kernel(
     sizes, a_hbm, lp_ref, linv_hbm, piv_hbm, out_ref,
     a_ref, linv_ref, piv_ref,
-    rs_src, rs_dst, x_buf, t_buf, d_top, lf, z1, base,
+    rs_src, rs_dst, x_buf, t_buf, d_top, d_part, lt, lf, z1, base,
     rs_s, rs_r, ag_s, ag_r, sc_s, sc_r, ta_s, ta_r, tf_s, tf_r,
-    lx_s, lx_r, lz_s, lz_r, lc_s, lc_r, own_sem, in_sem,
+    lx_s, lx_r, lz_s, lz_r, lc_s, lc_r, lt_s, lt_r, own_sem, in_sem,
 ):
     rows_n, nz, nxh, nc, nb = sizes
     chunk = nb // rows_n
@@ -80,7 +92,7 @@
         pl.semaphore_signal(barrier, inc=1, device_id={"prow": row_peer(d)}, device_id_type=MESH)
     for d in range(1, nxh):
         pl.semaphore_signal(barrier, inc=1, device_id={"pcol": xh_peer(d)}, device_id_type=MESH)
-    for d in (1, -1, 2, -2):
+    for d in range(1, nz):
         pl.semaphore_signal(barrier, inc=1, device_id={"pcol": z_peer(d)}, device_id_type=MESH)
     pl.semaphore_signal(barrier, inc=1, device_id={"pcol": partner}, device_id_type=MESH)
 
@@ -124,20 +136,107 @@
     loads[1].wait()
     rs_src[0] = pick(col0).reshape(rows_n, chunk, -1)
 
-    pl.semaphore_wait(barrier, (rows_n - 1) + (nxh - 1) + 4 + 1)
+    pl.semaphore_wait(barrier, (rows_n - 1) + (nxh - 1) + (nz - 1) + 1)
 
     waits = []
 
-    lx = []
-    for s in range(2):
-        for d in range(1, nxh):
+    def panel_start(s):
+        copies = []
+        for d in sorted(range(1, nxh), key=lambda d: -min(d, nxh - d)):
             copy = send(
                 lp_ref.at[s], lf.at[s, z * nxh + xh, core], lx_s.at[s, d], lx_r.at[s, d],
                 pcol=xh_peer(d),
             )
             copy.start()
-            lx.append(copy)
-    waits += lx
+            copies.append(copy)
+        waits.extend(copies)
+        return copies
+
+    lx0 = panel_start(0)
+
+    first_top = nb // chunk
+    top_col = first_top + me
+    in_line = (z == top_col // (nxh * nc)) & (core == lax.rem(top_col, nc))
+    at_source = in_line & (xh == lax.rem(top_col // nc, nxh))
+    target = col - first_top
+
+    def lt_copy(n, stage, **where):
+        return send(lt, lt, lt_s.at[n], lt_r.at[stage], **where)
+
+    lt_x = [lt_copy(d, 1, pcol=xh_peer(d)) for d in range(1, nxh)]
+    lt_z = [lt_copy(nxh + d - 1, 2, pcol=z_peer(d)) for d in range(1, nz)]
+    lt_c = lt_copy(nxh + nz - 1, 3, pcol=partner)
+    lt_out = is_root & (target > 0) & (target < rows_n)
+    lt_first = send(lp_ref.at[0], lt, lt_s.at[0], lt_r.at[0], prow=lax.rem(target + rows_n, rows_n))
+    lt_own = pltpu.make_async_copy(lp_ref.at[0], lt, in_sem.at[3])
+
+    def top_panel_first():
+        @pl.when(lt_out)
+        def _():
+            lt_first.start()
+
+        @pl.when(is_root & at_source)
+        def _():
+            lt_own.start()
+
+    def top_panel_x():
+        @pl.when(is_root & at_source)
+        def _():
+            lt_own.wait()
+
+        @pl.when(jnp.logical_not(is_root) & at_source)
+        def _():
+            lt_first.wait_recv()
+
+        @pl.when(at_source)
+        def _():
+            for copy in lt_x:
+                copy.start()
+
+    def top_panel_z():
+        @pl.when(in_line & jnp.logical_not(at_source))
+        def _():
+            lt_x[0].wait_recv()
+
+        @pl.when(in_line)
+        def _():
+            for copy in lt_z:
+                copy.start()
+
+    same_core = core == lax.rem(top_col, nc)
+
+    def top_panel_core():
+        @pl.when(same_core & jnp.logical_not(in_line))
+        def _():
+            lt_z[0].wait_recv()
+
+        @pl.when(same_core)
+        def _():
+            lt_c.start()
+
+    def top_panel_finish():
+        @pl.when(jnp.logical_not(same_core))
+        def _():
+            lt_c.wait_recv()
+
+    def top_panel_sent():
+        @pl.when(lt_out)
+        def _():
+            lt_first.wait_send()
+
+        @pl.when(at_source)
+        def _():
+            for copy in lt_x:
+                copy.wait_send()
+
+        @pl.when(in_line)
+        def _():
+            for copy in lt_z:
+                copy.wait_send()
+
+        @pl.when(same_core)
+        def _():
+            lt_c.wait_send()
 
     def reduce_start(s):
         copies = []
@@ -194,32 +293,25 @@
         waits.append(copy)
         return copy
 
-    def scatter_copies(src, s):
+    def scatter_copies():
         copies = []
         for m in range(1, rows_n):
             rows = pl.ds(m * chunk, chunk)
-            copies.append(
-                send(
-                    src.at[rows], t_buf.at[s, m // 2, m % 2], sc_s.at[s, m], sc_r.at[s],
-                    prow=jnp.int32(m),
-                )
-            )
+            for s, (src, dst) in enumerate(
+                ((a_ref.at[rows], t_buf.at[0, m // 2, m % 2]), (d_top.at[rows], d_part))
+            ):
+                copies.append(send(src, dst, sc_s.at[s, m], sc_r.at[s], prow=jnp.int32(m)))
         return copies
 
     def scatter_wait(s):
-        piece = t_buf.at[s, y, x]
+        piece = (t_buf.at[0, y, x], d_part)[s]
 
         @pl.when(jnp.logical_not(is_root))
         def _():
             send(piece, piece, sc_s.at[s, 0], sc_r.at[s], prow=row_peer(1)).wait_recv()
 
     rs0 = reduce_start(0)
-
-    @pl.when(is_root)
-    def _():
-        own_t.start()
-        for copy in scatter_copies(a_ref, 0):
-            copy.start()
+    top_panel_first()
 
     z1[...] = pick(source(col1))
 
@@ -230,6 +322,7 @@
         moved = select(onehot.astype(BF16), a_ref[pl.ds(0, nb), :])
         swapped = jnp.max(onehot, axis=1, keepdims=True) > 0
         d_top[...] = jnp.where(swapped, moved, a_ref[pl.ds(nb, nb), :])
+        d_part[...] = d_top[pl.ds(0, chunk), :]
 
     turn = 1 - 2 * lax.rem(z, 2)
     routes = (
@@ -241,9 +334,9 @@
         group = lf.at[s, pl.ds(z_at(held) * nxh, nxh), core]
         return send(group, group, lz_s.at[s, q], lz_r.at[s, q], pcol=z_peer(there))
 
-    def panel_x(s):
+    def panel_x(s, lx):
         own[s].wait()
-        for copy in lx[s * (nxh - 1): (s + 1) * (nxh - 1)]:
+        for copy in lx:
             copy.wait_recv()
         copies = [z_copy(s, q) for q in (2, 3, 0, 1)]
         for copy in copies:
@@ -263,31 +356,44 @@
         return copies
 
     def panel_pass(s, copies):
-        for copy in copies:
+        copies[0].wait_recv()
+        copies[1].wait_recv()
+        passed = [z_copy(s, q) for q in (6, 4, 5)]
+        for copy in passed:
+            copy.start()
+        waits.extend(passed)
+        swaps = swap_start(s, (0, -2, 2))
+        copies[2].wait_recv()
+        copies[3].wait_recv()
+        return passed, swaps + swap_start(s, (-1, 1))
+
+    def panel_finish(s, copies, swaps):
+        for copy, d in zip(copies[1:] + copies[:1], (-3, 3, 4)):
             copy.wait_recv()
-        copies = [z_copy(s, q) for q in (6, 4, 5)]
-        for copy in copies:
-            copy.start()
-        waits.extend(copies)
-        return copies, swap_start(s, (0, -1, 1, -2, 2))
-
-    def panel_finish(s, copies, swaps):
-        for copy in copies:
-            copy.wait_recv()
-        swaps = swaps + swap_start(s, (4, -3, 3))
+            swaps = swaps + swap_start(s, (d,))
         for copy in swaps:
             copy.wait_recv()
 
     def tops(s):
         return t_buf[s].reshape(nb, -1)
 
-    lz0 = panel_x(0)
+    lz0 = panel_x(0, lx0)
 
     reduce_finish(0, rs0)
     ag0 = gather_start(0)
 
+    @pl.when(is_root)
+    def _():
+        own_t.start()
+        for copy in scatter_copies():
+            copy.start()
+
+    top_panel_x()
+    lx1 = panel_start(1)
+
     lz0 = panel_pass(0, lz0)
 
+    top_panel_z()
     scatter_wait(0)
 
     @pl.when(is_root)
@@ -300,83 +406,81 @@
         per = nz * nxh // blocks
         return lf[s, pl.ds(b * per, per)].reshape(nb, nb)
 
+    top_panel_core()
     panel_finish(0, *lz0)
-    lz1 = panel_x(1)
+    lz1 = panel_x(1, lx1)
     l_sel = None
     for b in range(blocks):
         onehot = (col1 == lane + (first + b * nb)).astype(F32).astype(BF16)
         part = select(onehot, factor(0, b))
         l_sel = part if l_sel is None else l_sel + part
+    l_sel = split(l_sel)
 
     for copy in ag0:
         copy.wait_recv()
     loads[2].wait()
     upper0 = matmul(linv_ref[0], x_buf[0])
-    rs_src[1] = (z1[...] - matmul(l_sel, upper0)).reshape(rows_n, chunk, -1)
+    upper0_parts = split(upper0)
+    rs_src[1] = (z1[...] - product(l_sel, upper0_parts)).reshape(rows_n, chunk, -1)
     rs1 = reduce_start(1)
 
-    @pl.when(is_root)
-    def _():
-        d_top[...] = d_top[...] - matmul(factor(0, 1), upper0)
-        t_buf[1, 0, 0] = d_top[pl.ds(0, chunk), :]
-        for copy in scatter_copies(d_top, 1):
-            copy.start()
+    top_panel_finish()
+    scatter_wait(1)
+    t_buf[1, y, x] = d_part[...] - product(split(lt[...]), upper0_parts)
+    ta1 = top_start(1)
 
     tf0 = top_forward(0, ta0)
+
+    for b in range(blocks):
+        rows = pl.ds(b * nb, nb)
+        base[rows, :] = product(split(factor(0, b)), upper0_parts)
+
     lz1 = panel_pass(1, lz1)
+
     tf0.wait_recv()
-
     for b in range(blocks):
-        here = sub + (first + b * nb)
-        hit = (here == row0).astype(F32)
+        rows = pl.ds(b * nb, nb)
+        hit = (sub + (first + b * nb) == row0).astype(F32)
         moved = select(hit.astype(BF16), tops(0))
         any_hit = jnp.max(hit, axis=1, keepdims=True) > 0
-        kept = jnp.where(any_hit, moved, a_ref[pl.ds(b * nb, nb), :])
-        base[pl.ds(b * nb, nb), :] = kept - matmul(factor(0, b), upper0)
+        base[rows, :] = jnp.where(any_hit, moved, a_ref[rows, :]) - base[rows, :]
 
     reduce_finish(1, rs1)
     ag1 = gather_start(1)
-    scatter_wait(1)
-    ta1 = top_start(1)
 
     panel_finish(1, *lz1)
 
     tf1 = top_forward(1, ta1)
+    tf1.wait_recv()
+    for b in range(blocks):
+        rows = pl.ds(b * nb, nb)
+        hit = (sub + (first + b * nb) == row1).astype(F32)
+        moved = select(hit.astype(BF16), tops(1))
+        any_hit = jnp.max(hit, axis=1, keepdims=True) > 0
+        base[rows, :] = jnp.where(any_hit, moved, base[rows, :])
 
     for copy in ag1:
         copy.wait_recv()
     upper1 = matmul(linv_ref[1], x_buf[1])
-    upper1_high = upper1.astype(BF16)
-    upper1_low = (upper1 - upper1_high.astype(F32)).astype(BF16)
-
-    tf1.wait_recv()
+    upper1_parts = split(upper1)
     for b in range(blocks):
-        here = sub + (first + b * nb)
-        hit = (here == row1).astype(F32)
-        moved = select(hit.astype(BF16), tops(1))
-        any_hit = jnp.max(hit, axis=1, keepdims=True) > 0
-        value = jnp.where(any_hit, moved, base[pl.ds(b * nb, nb), :])
-        left = factor(1, b)
-        high = left.astype(BF16)
-        low = (left - high.astype(F32)).astype(BF16)
-        change = jnp.dot(high, upper1_low, preferred_element_type=F32)
-        change = change + jnp.dot(low, upper1_high, preferred_element_type=F32)
-        change = change + jnp.dot(high, upper1_high, preferred_element_type=F32)
-        value = value - change
+        rows = pl.ds(b * nb, nb)
+        value = base[rows, :] - product(split(factor(1, b)), upper1_parts)
         if b == 0:
             value = jnp.where(is_root, upper0, value)
         if b == 1:
             value = jnp.where(is_root, upper1, value)
-        out_ref[pl.ds(b * nb, nb), :] = value
+        out_ref[rows, :] = value
 
     for copy in waits:
         copy.wait_send()
 
+    top_panel_sent()
+
     @pl.when(is_root)
     def _():
-        for s, src in ((0, a_ref), (1, d_top)):
-            for copy in scatter_copies(src, s):
-                copy.wait_send()
+        for copy in scatter_copies():
+            copy.wait_send()
 
 
 def per_device(split, rows_n, matrix, l_panels, l_inverse, pivots):
@@ -390,7 +494,7 @@
     return pl.pallas_call(
         functools.partial(kernel, (rows_n, nz, nxh, nc, nb)),
         out_shape=jax.ShapeDtypeStruct(matrix.shape, F32),
-        in_specs=[pl.BlockSpec(memory_space=pl.ANY)] * 4,
+        in_specs=[pl.BlockSpec(memory_space=pltpu.HBM)] * 4,
         out_specs=vmem,
         scratch_shapes=[
             pltpu.VMEM(matrix.shape, F32),
@@ -401,6 +505,8 @@
             pltpu.VMEM((2, nb, cols_dev), F32),
             pltpu.VMEM((2, rows_n // 2, 2, chunk, cols_dev), F32),
             pltpu.VMEM((nb, cols_dev), F32),
+            pltpu.VMEM((chunk, cols_dev), F32),
+            pltpu.VMEM((part, nb), F32),
             pltpu.VMEM((2, nz * nxh, nc, part, nb), F32),
             pltpu.VMEM((nb, cols_dev), F32),
             pltpu.VMEM((rows_dev, cols_dev), F32),
@@ -412,12 +518,16 @@
             dma((2, nxh)), dma((2, nxh)),
             dma((2, nz)), dma((2, nz)),
             dma((2, nz)), dma((2, nz)),
-            dma((3,)), dma((3,)),
+            dma((nxh + nz,)), dma((4,)),
+            dma((3,)), dma((4,)),
         ],
         compiler_params=pltpu.CompilerParams(
-            collective_id=0, has_side_effects=True, vmem_limit_bytes=48 * 1024 * 1024
+            collective_id=0, has_side_effects=True, vmem_limit_bytes=VMEM_LIMIT
         ),
-    )(matrix, l_panels, l_inverse, pivots)
+    )(*[
+        pltpu.with_memory_space_constraint(v, pltpu.HBM)
+        for v in (matrix, l_panels, l_inverse, pivots)
+    ])
 
 
 def solution(mesh):

time: 75.1 us -> 65.5 us (0.87)
  Pallas kernels: 70.1 us -> 63.5 us
  local copies, waits for them, and re-layouts: 4.68 us -> 0.97 us
    pallas_call x1, Pallas kernels: 70.1 us -> 63.5 us  [per_device(): pl.pallas_call(functools.partial(kernel, (rows_n, nz, nxh, nc, nb)), out_...]
    unnamed x9 -> x1, local copies, waits for them, and re-layouts: 4.68 us -> 0.97 us
where the time goes in v3:
time: 65.5 us; the launch traced here: 64.5 us
  Pallas kernels  63.5 us (97%)
  local copies, waits for them, and re-layouts  0.97 us (1%)
    pallas_call x1, Pallas kernels, per_device(): pl.pallas_call(functools.partial(kernel, (rows_n, nz, nxh, nc, nb)), out_...  63.5 us

profile of v3, /device:TPU:1, one launch (start us, length us, event | category | flops | bytes accessed | tf_op | source)
XLA Modules:
  0.0 64.5 jit_solution(16617576567523138712)
XLA Ops:
  0.0 63.5 %shard_map.46 = f32[1024,256]{1,0:T(8,128)S(1)} custom-call(f32[1024,256]{1,0:T(8,128)} %a_hbm.1, f32[2,16,256]{2,1,0:T(8,128)} %lp_ref.1, f32[2,256,256]{2,1,0:T(8,128)} %linv_hbm.1, s32[2,256]{1,0:T(2,128)} %piv_hbm.1), custom_call_target="tpu_custom_call" | custom-call | tf_op jit(solution)/shard_map/pallas_call | solution.py:494
  63.5 1.0 %copy.6 = f32[1024,256]{1,0:T(8,128)} copy(f32[1024,256]{1,0:T(8,128)S(1)} %shard_map.46) | data formatting | bytes 2097152

commit v4 on v3

--- a/solution.py
+++ b/solution.py
@@ -87,6 +87,12 @@
         )
         return copy
 
+    def arrived(ref, sem):
+        send(ref, ref, sem, sem, pcol=partner).wait_recv()
+
+    def sent(ref, sem):
+        send(ref, ref, sem, sem, pcol=partner).wait_send()
+
     barrier = pltpu.get_barrier_semaphore()
     for d in range(1, rows_n):
         pl.semaphore_signal(barrier, inc=1, device_id={"prow": row_peer(d)}, device_id_type=MESH)
@@ -138,21 +144,63 @@
 
     pl.semaphore_wait(barrier, (rows_n - 1) + (nxh - 1) + (nz - 1) + 1)
 
-    waits = []
-
     def panel_start(s):
-        copies = []
+        copies = {}
         for d in sorted(range(1, nxh), key=lambda d: -min(d, nxh - d)):
-            copy = send(
-                lp_ref.at[s], lf.at[s, z * nxh + xh, core], lx_s.at[s, d], lx_r.at[s, d],
+            copies[d] = send(
+                lp_ref.at[s], lf.at[s, z * nxh + xh, core], lx_s.at[s], lx_r.at[s, d],
                 pcol=xh_peer(d),
             )
-            copy.start()
-            copies.append(copy)
-        waits.extend(copies)
+            copies[d].start()
         return copies
 
+    turn = 1 - 2 * lax.rem(z, 2)
+    routes = (
+        (0, 1), (0, -1), (0, 2), (0, -2), (-2, 1), (2, -1), (-2 * turn, 2 * turn)
+    )
+
+    slots = sorted(range(nxh), key=lambda d: min(d, nxh - d))
+
+    def z_start(s, d, kinds):
+        copies = {}
+        for q in kinds:
+            held, there = routes[q]
+            piece = lf.at[s, z_at(held) * nxh + lax.rem(xh + d, nxh), core]
+            n = {0: nxh, 1: nxh, 2: d, 3: d}.get(q, nxh + q - 3)
+            send(piece, piece, lz_s.at[s], lz_r.at[s, n], pcol=z_peer(there)).start()
+
+    def panel_own(s):
+        own[s].wait()
+        z_start(s, 0, (2, 3))
+
+    def panel_x(s, lx):
+        for d in slots[1:]:
+            lx[nxh - d].wait_recv()
+            z_start(s, d, (2, 3))
+        for d in slots:
+            z_start(s, d, (0, 1))
+
+    def swap_start(s, offsets):
+        for d in offsets:
+            group = lf.at[s, pl.ds(z_at(d) * nxh, nxh), core]
+            send(group, group, lc_s.at[s], lc_r.at[s], pcol=partner).start()
+
+    def panel_pass(s):
+        for d in slots:
+            arrived(lf.at[s, pl.ds(0, 2), 0], lz_r.at[s, d])
+            z_start(s, d, (6, 4, 5))
+        swap_start(s, (0, -2, 2))
+        arrived(lf.at[s, pl.ds(0, 2 * nxh), 0], lz_r.at[s, nxh])
+        swap_start(s, (-1, 1))
+
+    def panel_finish(s):
+        for q, d in ((4, -3), (5, 3), (6, 4)):
+            arrived(lf.at[s, pl.ds(0, nxh), 0], lz_r.at[s, nxh + q - 3])
+            swap_start(s, (d,))
+        arrived(lf.at[s, :, 0], lc_r.at[s])
+
     lx0 = panel_start(0)
+    panel_own(0)
 
     first_top = nb // chunk
     top_col = first_top + me
@@ -160,12 +208,12 @@
     at_source = in_line & (xh == lax.rem(top_col // nc, nxh))
     target = col - first_top
 
-    def lt_copy(n, stage, **where):
-        return send(lt, lt, lt_s.at[n], lt_r.at[stage], **where)
-
-    lt_x = [lt_copy(d, 1, pcol=xh_peer(d)) for d in range(1, nxh)]
-    lt_z = [lt_copy(nxh + d - 1, 2, pcol=z_peer(d)) for d in range(1, nz)]
-    lt_c = lt_copy(nxh + nz - 1, 3, pcol=partner)
+    def lt_copy(stage, **where):
+        return send(lt, lt, lt_s.at[stage], lt_r.at[stage], **where)
+
+    lt_x = [lt_copy(1, pcol=xh_peer(d)) for d in range(1, nxh)]
+    lt_z = [lt_copy(2, pcol=z_peer(d)) for d in range(1, nz)]
+    lt_c = lt_copy(3, pcol=partner)
     lt_out = is_root & (target > 0) & (target < rows_n)
     lt_first = send(lp_ref.at[0], lt, lt_s.at[0], lt_r.at[0], prow=lax.rem(target + rows_n, rows_n))
     lt_own = pltpu.make_async_copy(lp_ref.at[0], lt, in_sem.at[3])
@@ -226,81 +274,62 @@
 
         @pl.when(at_source)
         def _():
-            for copy in lt_x:
-                copy.wait_send()
+            sent(lf.at[0, pl.ds(0, nxh - 1), 0], lt_s.at[1])
 
         @pl.when(in_line)
         def _():
-            for copy in lt_z:
-                copy.wait_send()
+            sent(lf.at[0, pl.ds(0, nz - 1), 0], lt_s.at[2])
 
         @pl.when(same_core)
         def _():
             lt_c.wait_send()
 
     def reduce_start(s):
-        copies = []
         for d in far:
-            copy = send(
-                rs_src.at[s, row_peer(d)], rs_dst.at[s, d], rs_s.at[s, d], rs_r.at[s, d],
+            send(
+                rs_src.at[s, row_peer(d)], rs_dst.at[s, d], rs_s.at[s], rs_r.at[s],
                 prow=row_peer(d),
-            )
-            copy.start()
-            copies.append(copy)
-        waits.extend(copies)
-        return copies
-
-    def reduce_finish(s, copies):
+            ).start()
+
+    def reduce_finish(s):
+        arrived(rs_dst.at[s, pl.ds(1, rows_n - 1)], rs_r.at[s])
         total = rs_src[s, me]
-        for d, copy in reversed(list(zip(far, copies))):
-            copy.wait_recv()
+        for d in range(1, rows_n):
             total = total + rs_dst[s, d]
         mine = pl.ds(pl.multiple_of(me * chunk, chunk), chunk)
         x_buf[s, mine, :] = total
 
+    others = pl.ds(0, (rows_n - 1) * chunk)
+
     def gather_start(s):
         mine = pl.ds(pl.multiple_of(me * chunk, chunk), chunk)
-        copies = []
         for d in far:
-            copy = send(
-                x_buf.at[s, mine], x_buf.at[s, mine], ag_s.at[s, d], ag_r.at[s, d],
-                prow=row_peer(d),
-            )
-            copy.start()
-            copies.append(copy)
-        waits.extend(copies)
-        return copies
+            send(
+                x_buf.at[s, mine], x_buf.at[s, mine], ag_s.at[s], ag_r.at[s], prow=row_peer(d)
+            ).start()
 
     def top_start(s):
-        copies = []
         for d in sorted(range(1, ny), key=lambda d: -min(d, ny - d)):
             piece = t_buf.at[s, y, x]
-            copy = send(
-                piece, piece, ta_s.at[s, d], ta_r.at[s, d], prow=lax.rem(y + d, ny) * 2 + x
-            )
-            copy.start()
-            copies.append(copy)
-        waits.extend(copies)
-        return copies
-
-    def top_forward(s, copies):
-        for copy in copies:
-            copy.wait_recv()
+            send(
+                piece, piece, ta_s.at[s], ta_r.at[s], prow=lax.rem(y + d, ny) * 2 + x
+            ).start()
+
+    def top_forward(s):
+        arrived(t_buf.at[s, pl.ds(0, ny - 1), 0], ta_r.at[s])
         copy = send(
             t_buf.at[s, :, x], t_buf.at[s, :, x], tf_s.at[s], tf_r.at[s], prow=y * 2 + 1 - x
         )
         copy.start()
-        waits.append(copy)
         return copy
 
-    def scatter_copies():
+    def scatter_copies(s):
         copies = []
-        for m in range(1, rows_n):
+        for m in sorted(range(1, rows_n), key=lambda m: -min(m, rows_n - m)):
             rows = pl.ds(m * chunk, chunk)
-            for s, (src, dst) in enumerate(
-                ((a_ref.at[rows], t_buf.at[0, m // 2, m % 2]), (d_top.at[rows], d_part))
-            ):
-                copies.append(send(src, dst, sc_s.at[s, m], sc_r.at[s], prow=jnp.int32(m)))
+            src = (a_ref, d_top)[s].at[rows]
+            dst = (t_buf.at[0, m // 2, m % 2], d_part)[s]
+            copies.append(send(src, dst, sc_s.at[s], sc_r.at[s], prow=jnp.int32(m)))
         return copies
 
     def scatter_wait(s):
@@ -308,9 +337,9 @@
 
         @pl.when(jnp.logical_not(is_root))
         def _():
-            send(piece, piece, sc_s.at[s, 0], sc_r.at[s], prow=row_peer(1)).wait_recv()
-
-    rs0 = reduce_start(0)
+            arrived(piece, sc_r.at[s])
+
+    reduce_start(0)
     top_panel_first()
 
     z1[...] = pick(source(col1))
@@ -324,74 +353,29 @@
         d_top[...] = jnp.where(swapped, moved, a_ref[pl.ds(nb, nb), :])
         d_part[...] = d_top[pl.ds(0, chunk), :]
 
-    turn = 1 - 2 * lax.rem(z, 2)
-    routes = (
-        (0, 1), (0, -1), (0, 2), (0, -2), (-2, 1), (2, -1), (-2 * turn, 2 * turn)
-    )
-
-    def z_copy(s, q):
-        held, there = routes[q]
-        group = lf.at[s, pl.ds(z_at(held) * nxh, nxh), core]
-        return send(group, group, lz_s.at[s, q], lz_r.at[s, q], pcol=z_peer(there))
-
-    def panel_x(s, lx):
-        own[s].wait()
-        for copy in lx:
-            copy.wait_recv()
-        copies = [z_copy(s, q) for q in (2, 3, 0, 1)]
-        for copy in copies:
-            copy.start()
-        waits.extend(copies)
-        return copies
-
-    def swap_start(s, offsets):
-        copies = []
-        for d in offsets:
-            group = lf.at[s, pl.ds(z_at(d) * nxh, nxh), core]
-            copies.append(
-                send(group, group, lc_s.at[s, d + 3], lc_r.at[s, d + 3], pcol=partner)
-            )
-            copies[-1].start()
-        waits.extend(copies)
-        return copies
-
-    def panel_pass(s, copies):
-        copies[0].wait_recv()
-        copies[1].wait_recv()
-        passed = [z_copy(s, q) for q in (6, 4, 5)]
-        for copy in passed:
-            copy.start()
-        waits.extend(passed)
-        swaps = swap_start(s, (0, -2, 2))
-        copies[2].wait_recv()
-        copies[3].wait_recv()
-        return passed, swaps + swap_start(s, (-1, 1))
-
-    def panel_finish(s, copies, swaps):
-        for copy, d in zip(copies[1:] + copies[:1], (-3, 3, 4)):
-            copy.wait_recv()
-            swaps = swaps + swap_start(s, (d,))
-        for copy in swaps:
-            copy.wait_recv()
-
     def tops(s):
         return t_buf[s].reshape(nb, -1)
 
-    lz0 = panel_x(0, lx0)
-
-    reduce_finish(0, rs0)
-    ag0 = gather_start(0)
+    panel_x(0, lx0)
+
+    reduce_finish(0)
+    gather_start(0)
 
     @pl.when(is_root)
     def _():
         own_t.start()
-        for copy in scatter_copies():
+        for copy in scatter_copies(0):
             copy.start()
 
     top_panel_x()
     lx1 = panel_start(1)
 
-    lz0 = panel_pass(0, lz0)
+    panel_pass(0)
+
+    @pl.when(is_root)
+    def _():
+        for copy in scatter_copies(1):
+            copy.start()
 
     top_panel_z()
     scatter_wait(0)
@@ -400,15 +384,16 @@
     def _():
         own_t.wait()
 
-    ta0 = top_start(0)
+    top_start(0)
 
     def factor(s, b):
         per = nz * nxh // blocks
         return lf[s, pl.ds(b * per, per)].reshape(nb, nb)
 
     top_panel_core()
-    panel_finish(0, *lz0)
-    lz1 = panel_x(1, lx1)
+    panel_finish(0)
+    panel_own(1)
+    panel_x(1, lx1)
     l_sel = None
     for b in range(blocks):
         onehot = (col1 == lane + (first + b * nb)).astype(F32).astype(BF16)
@@ -416,26 +401,31 @@
         l_sel = part if l_sel is None else l_sel + part
     l_sel = split(l_sel)
 
-    for copy in ag0:
-        copy.wait_recv()
+    arrived(x_buf.at[0, others], ag_r.at[0])
     loads[2].wait()
     upper0 = matmul(linv_ref[0], x_buf[0])
     upper0_parts = split(upper0)
     rs_src[1] = (z1[...] - product(l_sel, upper0_parts)).reshape(rows_n, chunk, -1)
-    rs1 = reduce_start(1)
+    reduce_start(1)
 
     top_panel_finish()
     scatter_wait(1)
     t_buf[1, y, x] = d_part[...] - product(split(lt[...]), upper0_parts)
-    ta1 = top_start(1)
-
-    tf0 = top_forward(0, ta0)
+    top_start(1)
+
+    tf0 = top_forward(0)
 
     for b in range(blocks):
         rows = pl.ds(b * nb, nb)
         base[rows, :] = product(split(factor(0, b)), upper0_parts)
 
-    lz1 = panel_pass(1, lz1)
+    panel_pass(1)
+
+    reduce_finish(1)
+    gather_start(1)
+    tf1 = top_forward(1)
+
+    panel_finish(1)
 
     tf0.wait_recv()
     for b in range(blocks):
@@ -445,12 +435,6 @@
         any_hit = jnp.max(hit, axis=1, keepdims=True) > 0
         base[rows, :] = jnp.where(any_hit, moved, a_ref[rows, :]) - base[rows, :]
 
-    reduce_finish(1, rs1)
-    ag1 = gather_start(1)
-
-    panel_finish(1, *lz1)
-
-    tf1 = top_forward(1, ta1)
     tf1.wait_recv()
     for b in range(blocks):
         rows = pl.ds(b * nb, nb)
@@ -459,8 +443,7 @@
         any_hit = jnp.max(hit, axis=1, keepdims=True) > 0
         base[rows, :] = jnp.where(any_hit, moved, base[rows, :])
 
-    for copy in ag1:
-        copy.wait_recv()
+    arrived(x_buf.at[1, others], ag_r.at[1])
     upper1 = matmul(linv_ref[1], x_buf[1])
     upper1_parts = split(upper1)
     for b in range(blocks):
@@ -472,15 +455,22 @@
             value = jnp.where(is_root, upper1, value)
         out_ref[rows, :] = value
 
-    for copy in waits:
-        copy.wait_send()
+    for s in range(2):
+        sent(lf.at[s, pl.ds(0, nxh - 1), 0], lx_s.at[s])
+        sent(lf.at[s, pl.ds(0, (nz - 1) * nxh), 0], lz_s.at[s])
+        sent(lf.at[s, :, 0], lc_s.at[s])
+        sent(rs_src.at[s, pl.ds(1, rows_n - 1)], rs_s.at[s])
+        sent(x_buf.at[s, others], ag_s.at[s])
+        sent(t_buf.at[s, pl.ds(0, ny - 1), 0], ta_s.at[s])
+    tf0.wait_send()
+    tf1.wait_send()
 
     top_panel_sent()
 
     @pl.when(is_root)
     def _():
-        for copy in scatter_copies():
-            copy.wait_send()
+        for s in range(2):
+            sent(d_top.at[others], sc_s.at[s])
 
 
 def per_device(split, rows_n, matrix, l_panels, l_inverse, pivots):
@@ -510,15 +500,10 @@
             pltpu.VMEM((2, nz * nxh, nc, part, nb), F32),
             pltpu.VMEM((nb, cols_dev), F32),
             pltpu.VMEM((rows_dev, cols_dev), F32),
-            dma((2, rows_n)), dma((2, rows_n)),
-            dma((2, rows_n)), dma((2, rows_n)),
-            dma((2, rows_n)), dma((2,)),
-            dma((2, rows_n)), dma((2, rows_n)),
-            dma((2,)), dma((2,)),
-            dma((2, nxh)), dma((2, nxh)),
-            dma((2, nz)), dma((2, nz)),
-            dma((2, nz)), dma((2, nz)),
-            dma((nxh + nz,)), dma((4,)),
+            dma((2,)), dma((2,)), dma((2,)), dma((2,)),
+            dma((2,)), dma((2,)), dma((2,)), dma((2,)), dma((2,)), dma((2,)),
+            dma((2,)), dma((2, nxh)), dma((2,)), dma((2, nxh + 4)), dma((2,)), dma((2,)),
+            dma((4,)), dma((4,)),
             dma((3,)), dma((4,)),
         ],
         compiler_params=pltpu.CompilerParams(

time: 65.5 us -> 61.8 us (0.944); the launches traced: 64.5 us -> 61.6 us
  Pallas kernels: 63.5 us -> 60.6 us
    pallas_call x1, Pallas kernels: 63.5 us -> 60.6 us  [per_device(): pl.pallas_call(functools.partial(kernel, (rows_n, nz, nxh, nc, nb)), out_...]
where the time goes in v4:
time: 61.8 us; the launch traced here: 61.6 us
  Pallas kernels  60.6 us (98%)
  local copies, waits for them, and re-layouts  0.97 us (2%)
    pallas_call x1, Pallas kernels, per_device(): pl.pallas_call(functools.partial(kernel, (rows_n, nz, nxh, nc, nb)), out_...  60.6 us

profile of v4, /device:TPU:1, one launch (start us, length us, event | category | flops | bytes accessed | tf_op | source)
XLA Modules:
  0.0 61.6 jit_solution(12706781898050632172)
XLA Ops:
  0.0 60.6 %shard_map.46 = f32[1024,256]{1,0:T(8,128)S(1)} custom-call(f32[1024,256]{1,0:T(8,128)} %a_hbm.1, f32[2,16,256]{2,1,0:T(8,128)} %lp_ref.1, f32[2,256,256]{2,1,0:T(8,128)} %linv_hbm.1, s32[2,256]{1,0:T(2,128)} %piv_hbm.1), custom_call_target="tpu_custom_call" | custom-call | tf_op jit(solution)/shard_map/pallas_call | solution.py:484
  60.6 1.0 %copy.6 = f32[1024,256]{1,0:T(8,128)} copy(f32[1024,256]{1,0:T(8,128)S(1)} %shard_map.46) | data formatting | bytes 2097152

commit v5 on v4

--- a/solution.py
+++ b/solution.py
@@ -378,6 +378,13 @@
             copy.start()
 
     top_panel_z()
+    def factor(s, b):
+        per = nz * nxh // blocks
+        return lf[s, pl.ds(b * per, per)].reshape(nb, nb)
+
+    top_panel_core()
+    panel_finish(0)
+
     scatter_wait(0)
 
     @pl.when(is_root)
@@ -386,12 +393,6 @@
 
     top_start(0)
 
-    def factor(s, b):
-        per = nz * nxh // blocks
-        return lf[s, pl.ds(b * per, per)].reshape(nb, nb)
-
-    top_panel_core()
-    panel_finish(0)
     panel_own(1)
     panel_x(1, lx1)
     l_sel = None
@@ -413,8 +414,6 @@
     t_buf[1, y, x] = d_part[...] - product(split(lt[...]), upper0_parts)
     top_start(1)
 
-    tf0 = top_forward(0)
-
     for b in range(blocks):
         rows = pl.ds(b * nb, nb)
         base[rows, :] = product(split(factor(0, b)), upper0_parts)
@@ -423,6 +422,7 @@
 
     reduce_finish(1)
     gather_start(1)
+    tf0 = top_forward(0)
     tf1 = top_forward(1)
 
     panel_finish(1)

time: 61.8 us -> 64.3 us (1.040); the launches traced: 61.6 us -> 63.1 us
  Pallas kernels: 60.6 us -> 62.2 us
    pallas_call x1, Pallas kernels: 60.6 us -> 62.2 us  [per_device(): pl.pallas_call(functools.partial(kernel, (rows_n, nz, nxh, nc, nb)), out_...]
where the time goes in v5:
time: 64.3 us; the launch traced here: 63.1 us
  Pallas kernels  62.2 us (97%)
  local copies, waits for them, and re-layouts  0.97 us (2%)
    pallas_call x1, Pallas kernels, per_device(): pl.pallas_call(functools.partial(kernel, (rows_n, nz, nxh, nc, nb)), out_...  62.2 us

profile of v5, /device:TPU:1, one launch (start us, length us, event | category | flops | bytes accessed | tf_op | source)
XLA Modules:
  0.0 63.1 jit_solution(18383485236801420961)
XLA Ops:
  0.0 62.2 %shard_map.46 = f32[1024,256]{1,0:T(8,128)S(1)} custom-call(f32[1024,256]{1,0:T(8,128)} %a_hbm.1, f32[2,16,256]{2,1,0:T(8,128)} %lp_ref.1, f32[2,256,256]{2,1,0:T(8,128)} %linv_hbm.1, s32[2,256]{1,0:T(2,128)} %piv_hbm.1), custom_call_target="tpu_custom_call" | custom-call | tf_op jit(solution)/shard_map/pallas_call | solution.py:484
  62.2 1.0 %copy.6 = f32[1024,256]{1,0:T(8,128)} copy(f32[1024,256]{1,0:T(8,128)S(1)} %shard_map.46) | data formatting | bytes 2097152
